TPU v7x, 128 devices: a whole 4x4x4 slice. The times are simulated.
128 devices in a mesh: rep: 32 (over z, x, y_hi), tp: 4 (over y_lo, core).
Axes of the slice: x: 4, y: 4 (y_hi: 2, y_lo: 2; y = y_hi * 2 + y_lo), z: 4, core: 2. Of those that a mesh axis runs over, the one named last changes fastest.
Arguments:
- weight: bfloat16 [32, 2048, 7168], P('rep', None, 'tp'), may hold values from -6 to 6
- tokens: bfloat16 [32, 2, 512, 2048], P('rep'), may hold values from -6 to 6
- cotangent: bfloat16 [32, 2, 512, 7168], P('rep', None, None, 'tp'), may hold values from -6 to 6
- batch_order: int32 [32, 2], P('rep'), may hold values from 0 to 1, each once within a row
- step_index: int32 [1], replicated, may hold values from 0 to 999
Outputs:
- averaged: bfloat16 [32, 2048, 7168], P('rep', None, 'tp')
- losses: float32 [32, 2], P('rep')
Inputs may be any that keep to these rules, and one draw needn't show every extreme that they name: `batch_order`: each row lists 0 to 1 once.
All inputs are finite; a program needn't handle non-finite values.
Results may differ from a plain program's by a relative error of at most 0.009.
Values may be sent and summed in bfloat16 or wider, within the bound.
A program may use at most 256 MiB of HBM per device.

v0:
```python
import jax
import jax.numpy as jnp
from jax import lax
from jax.sharding import PartitionSpec as P

FF = 7168


beta_first = 0.9
beta_second = 0.95
learn_rate = 0.05
decay_rate = 0.1
adam_eps = 1e-05
norm_eps = 1e-06


def copy_for_each(array, axis):
    copies = jnp.broadcast_to(array, (lax.axis_size(axis), *array.shape))
    return lax.all_to_all(copies, axis, split_axis=0, concat_axis=0, tiled=True)


def taken_together(array, axis):
    everything = copy_for_each(array, axis)
    return jnp.sum(everything, axis=0)


def together(arrays, axis):
    line, at, done = (jnp.concatenate([a.reshape(-1) for a in arrays]), 0, [])
    total = taken_together(line, axis)
    for a in arrays:
        done.append(total[at : at + a.size].reshape(a.shape))
        at += a.size
    return tuple(done)


def shifted_2(array, axis, by):
    devices = lax.axis_size(axis)
    return lax.ppermute(array, axis, [(i, (i + by) % devices) for i in range(devices)])


def run_chain(weight, tokens, cotangent, order, combine_stats):
    width_scale = weight.shape[0] ** (-0.5)
    master = weight.astype(jnp.float32)
    moment = jnp.zeros(master.shape, jnp.float32)
    second = jnp.zeros(master.shape, jnp.float32)
    losses = []
    for local_step in range(tokens.shape[0]):
        chosen = order[local_step]
        inputs = lax.dynamic_index_in_dim(tokens, chosen, 0, keepdims=False)
        target = lax.dynamic_index_in_dim(cotangent, chosen, 0, keepdims=False).astype(jnp.float32)
        current = master.astype(jnp.bfloat16)
        hidden = jnp.dot(inputs, current, preferred_element_type=jnp.float32) * width_scale
        squares, inner = combine_stats(
            jnp.sum(hidden * hidden, axis=1), jnp.sum(target * hidden, axis=1)
        )
        radius = jnp.sqrt(squares / FF + norm_eps)
        losses.append(jnp.mean(inner / radius))
        token_count = inputs.shape[0]
        grad_rows = (
            target / radius[:, None] - hidden * (inner / (FF * radius**3))[:, None]
        ) / token_count
        grad_rows = grad_rows.astype(jnp.bfloat16)
        gradient = (
            lax.dot_general(
                inputs, grad_rows, (((0,), (0,)), ((), ())), preferred_element_type=jnp.float32
            )
            * width_scale
        )
        moment = beta_first * moment + (1.0 - beta_first) * gradient
        second = beta_second * second + (1.0 - beta_second) * gradient * gradient
        moment_hat = moment / (1.0 - beta_first ** (local_step + 1))
        second_hat = second / (1.0 - beta_second ** (local_step + 1))
        master = master - learn_rate * (
            moment_hat / (jnp.sqrt(second_hat) + adam_eps) + decay_rate * master
        )
    return (master.astype(jnp.bfloat16), jnp.stack(losses))


def own_stats(squares, inner):
    return together((squares, inner), "tp")


def shards(weight, tokens, cotangent, batch_order, step_index):
    levels = lax.axis_size("rep").bit_length() - 1
    hop_level = step_index[0] % levels
    final_weight, losses = run_chain(weight[0], tokens[0], cotangent[0], batch_order[0], own_stats)

    def make_final(exponent):

        def shifted():
            return shifted_2(final_weight, "rep", 2**exponent)

        return shifted

    peer_weight = lax.switch(hop_level, [make_final(exponent) for exponent in range(levels)])
    averaged = ((final_weight.astype(jnp.float32) + peer_weight.astype(jnp.float32)) * 0.5).astype(
        jnp.bfloat16
    )
    return (averaged[None], losses[None])


def solution(mesh):
    placed = (
        P("rep", None, "tp"),
        P("rep", None, None, None),
        P("rep", None, None, "tp"),
        P("rep", None),
        P(),
    )
    return jax.shard_map(
        shards,
        mesh=mesh,
        in_specs=placed,
        out_specs=(P("rep", None, "tp"), P("rep", None)),
        check_vma=False,
    )
```

profile of v0, /device:TPU:1, one launch (start us, length us, event | category | flops | bytes accessed | tf_op | source)
XLA Modules:
  0.0 273.1 jit_solution(11688471581883499157)
XLA Ops:
  0.6 1.3 fusion.55
  3.9 0.0 slice-start
  3.9 10.2 %multiply_reduce_fusion.1 = (f32[512]{0:T(512)S(1)}, f32[512]{0:T(512)S(1)}, f32[512,1792]{1,0:T(8,128)}) fusion(bf16[1,2,512,1792]{3,2,1,0:T(8,128)(2,1)} %param.12, s32[]{:T(128)S(6)} %select_n.17, bf16[1,2048,1792]{2,1,0:T(8,128)(2,1)} %param.10, bf16[1,2,512,2048]{3,2,1,0:T(8,128)(2,1)} %param.11), kind=kOutput, calls=%fused_computation.25 | convolution fusion | flops 3763600384 | bytes 14947328 | tf_op jit(solution)/shard_map/dot_general | solution.py:52
  14.1 0.6 broadcast_in_dim.16
  14.7 4.6 %all-to-all-start = ((f32[4,1,1024]{2,1,0:T(1,128)}), f32[4,1,1024]{2,1,0:T(1,128)S(1)}, u32[]{:S(2)}, u32[]{:S(2)}) async-start(f32[4,1,1024]{2,1,0:T(1,128)} %broadcast_in_dim.16), calls=%async_computation | async-start | bytes 32768 | tf_op jit(solution)/shard_map/all_to_all | solution.py:19
  21.2 1.2 all-to-all-done
  22.4 0.6 divide_reduce_fusion.1
  23.1 0.0 slice-start.1
  23.1 0.0 copy-start.1
  23.1 0.0 copy-start.2
  23.1 12.9 %fusion.17 = f32[2048,1792]{1,0:T(8,128)} fusion(bf16[1,2,512,2048]{3,2,1,0:T(8,128)(2,1)} %param.11, s32[]{:T(128)S(6)} %select_n.17, f32[512,1792]{1,0:T(8,128)} %get-tuple-element.31, f32[512]{0:T(512)S(1)} %get-tuple-element.24, f32[512]{0:T(512)S(1)} %get-tuple-element.25, bf16[1,2,512,1792]{3,2,1,0:T(8,128)(2,1)} %param.12), kind=kOutput, calls=%fused_computation.28 | convolution fusion | flops 3763601408 | bytes 22287360 | tf_op jit(solution)/shard_map/dot_general | solution.py:64
  35.9 0.0 slice-done
  35.9 0.0 slice-done.1
  35.9 0.0 copy-done.1
  35.9 0.0 copy-done.2
  36.0 18.7 %multiply_reduce_fusion = (f32[512]{0:T(512)S(1)}, f32[512]{0:T(512)S(1)}, f32[512,1792]{1,0:T(8,128)}) fusion(bf16[1,2,512,1792]{3,2,1,0:T(8,128)(2,1)S(1)} %copy-done.2, s32[]{:T(128)S(6)} %select_n.18, f32[2048,1792]{1,0:T(8,128)} %fusion.17, bf16[1,2048,1792]{2,1,0:T(8,128)(2,1)S(1)} %bitcast.51, bf16[1,2,512,2048]{3,2,1,0:T(8,128)(2,1)S(1)} %copy-done.1), kind=kOutput, calls=%fused_computation.24 | convolution fusion | flops 3811310592 | bytes 29627392 | tf_op jit(solution)/shard_map/dot_general | solution.py:52
  54.7 0.6 broadcast_in_dim.17
  55.3 3.9 %all-to-all-start.1 = ((f32[4,1,1024]{2,1,0:T(1,128)}), f32[4,1,1024]{2,1,0:T(1,128)S(1)}, u32[]{:S(2)}, u32[]{:S(2)}) async-start(f32[4,1,1024]{2,1,0:T(1,128)} %broadcast_in_dim.17), calls=%async_computation.1 | async-start | bytes 32768 | tf_op jit(solution)/shard_map/all_to_all | solution.py:19
  60.5 1.8 all-to-all-done.1
  62.4 0.6 divide_reduce_fusion
  63.7 31.6 %subtract_convert_fusion = bf16[2048,1792]{1,0:T(8,128)(2,1)S(1)} fusion(f32[2048,1792]{1,0:T(8,128)} %fusion.17, bf16[1,2,512,2048]{3,2,1,0:T(8,128)(2,1)} %param.11, s32[]{:T(128)S(6)} %select_n.18, f32[512,1792]{1,0:T(8,128)} %get-tuple-element.32, f32[512]{0:T(512)S(1)} %get-tuple-element.27, f32[512]{0:T(512)S(1)} %get-tuple-element.28, ...), kind=kOutput, calls=%fused_computation.5 | convolution fusion | flops 3870031872 | bytes 36967424 | tf_op jit(solution)/shard_map/dot_general | solution.py:64
  95.3 0.0 copy-start
  95.3 3.0 %copy-done = bf16[2048,1792]{1,0:T(8,128)(2,1)} copy-done((bf16[2048,1792]{1,0:T(8,128)(2,1)}, bf16[2048,1792]{1,0:T(8,128)(2,1)S(1)}, u32[]{:S(2)}) %copy-start) | copy-done | bytes 7340056
  98.3 163.8 %conditional.4 = (bf16[2048,1792]{1,0:T(8,128)(2,1)}) conditional(s32[]{:T(128)} %clamp.3, bf16[2048,1792]{1,0:T(8,128)(2,1)S(1)} %subtract_convert_fusion, bf16[2048,1792]{1,0:T(8,128)(2,1)S(1)} %subtract_convert_fusion, bf16[2048,1792]{1,0:T(8,128)(2,1)S(1)} %subtract_convert_fusion, ...), branch_computations={%region_6.7_spmd, %region_7.8_spmd, %region_8.9_spmd, %region_9.10... | conditional | bytes 29360176
  98.3 1.3 collective-permute-start.1
  99.6 162.5 %collective-permute-done.1 = bf16[2048,1792]{1,0:T(8,128)(2,1)} collective-permute-done((bf16[2048,1792]{1,0:T(8,128)(2,1)S(1)}, bf16[2048,1792]{1,0:T(8,128)(2,1)}, u32[]{:S(2)}, u32[]{:S(2)}) %collective-permute-start.1) | collective-permute-done | bytes 7340064 | tf_op jit(solution)/shard_map/cond/branch_1_fun/ppermute | solution.py:38
  262.1 10.5 %fusion.2 = bf16[1,2048,1792]{2,1,0:T(8,128)(2,1)} fusion(bf16[2048,1792]{1,0:T(8,128)(2,1)} %get-tuple-element.33, bf16[2048,1792]{1,0:T(8,128)(2,1)} %copy-done), kind=kLoop, calls=%fused_computation.7 | loop fusion | flops 18350080 | bytes 22020096 | tf_op jit(solution)/shard_map/broadcast_in_dim | solution.py:99
  272.6 0.6 maximum_bitcast_fusion
  (5 shorter events, 0.1 us)
Async XLA Ops:
  3.9 32.1 %slice-start = ((s8[7340032]{0:T(1024)(128)(4,1)}), s8[3145728]{0:T(1024)(128)(4,1)S(1)}, s32[]{:S(2)}) async-start(s8[7340032]{0:T(1024)(128)(4,1)} %bitcast.50), calls=%async_computation.2 | async-start | bytes 6291456
  14.7 7.7 %all-to-all-start = ((f32[4,1,1024]{2,1,0:T(1,128)}), f32[4,1,1024]{2,1,0:T(1,128)S(1)}, u32[]{:S(2)}, u32[]{:S(2)}) async-start(f32[4,1,1024]{2,1,0:T(1,128)} %broadcast_in_dim.16), calls=%async_computation | async-start | bytes 32768 | tf_op jit(solution)/shard_map/all_to_all | solution.py:19
  23.1 12.9 %slice-start.1 = ((s8[7340032]{0:T(1024)(128)(4,1)}), s8[4194304]{0:T(1024)(128)(4,1)S(1)}, s32[]{:S(2)}) async-start(s8[7340032]{0:T(1024)(128)(4,1)} %bitcast.50), calls=%async_computation.3 | async-start | bytes 8388608
  23.1 12.9 %copy-start.1 = (bf16[1,2,512,2048]{3,2,1,0:T(8,128)(2,1)S(1)}, bf16[1,2,512,2048]{3,2,1,0:T(8,128)(2,1)}, u32[]{:S(2)}) copy-start(bf16[1,2,512,2048]{3,2,1,0:T(8,128)(2,1)} %param.11) | copy-start | bytes 12582916
  23.1 12.9 %copy-start.2 = (bf16[1,2,512,1792]{3,2,1,0:T(8,128)(2,1)S(1)}, bf16[1,2,512,1792]{3,2,1,0:T(8,128)(2,1)}, u32[]{:S(2)}) copy-start(bf16[1,2,512,1792]{3,2,1,0:T(8,128)(2,1)} %param.12) | copy-start | bytes 11010052
  55.3 7.1 %all-to-all-start.1 = ((f32[4,1,1024]{2,1,0:T(1,128)}), f32[4,1,1024]{2,1,0:T(1,128)S(1)}, u32[]{:S(2)}, u32[]{:S(2)}) async-start(f32[4,1,1024]{2,1,0:T(1,128)} %broadcast_in_dim.17), calls=%async_computation.1 | async-start | bytes 32768 | tf_op jit(solution)/shard_map/all_to_all | solution.py:19
  95.3 3.1 %copy-start = (bf16[2048,1792]{1,0:T(8,128)(2,1)}, bf16[2048,1792]{1,0:T(8,128)(2,1)S(1)}, u32[]{:S(2)}) copy-start(bf16[2048,1792]{1,0:T(8,128)(2,1)S(1)} %subtract_convert_fusion) | copy-start | bytes 22020100
  98.3 163.8 %collective-permute-start.1 = (bf16[2048,1792]{1,0:T(8,128)(2,1)S(1)}, bf16[2048,1792]{1,0:T(8,128)(2,1)}, u32[]{:S(2)}, u32[]{:S(2)}) collective-permute-start(bf16[2048,1792]{1,0:T(8,128)(2,1)S(1)} %param.1), channel_id=1, source_target_pairs={{0,8},{4,12},{8,16},{12,20},{16,24},{20,28},{24,32},{28,36},{32,40... | collective-permute-start | bytes 22020104 | tf_op jit(solution)/shard_map/cond/branch_1_fun/ppermute | solution.py:38
where the time goes:
time: 275 us; the launch traced here: 273 us
  waiting for transfers between devices  165 us (60%)
  matrix products  73.4 us (27%)
  other arithmetic  12.4 us (5%)
  starting transfers between devices  9.84 us (4%)
  between operations  6.49 us (2%)
  local copies, waits for them, and re-layouts  5.59 us (2%)
    ppermute x1, waiting for transfers between devices, shifted_2(): lax.ppermute(array, axis, [(i, (i + by) % devices) for i in range(devices)])  162 us
    dot_general x2, matrix products, run_chain(): lax.dot_general(inputs, grad_rows, (((0,), (0,)), ((), ())), preferred_el...  44.4 us
    dot_general x2, matrix products, run_chain(): jnp.dot(inputs, current, preferred_element_type=jnp.float32) * width_scale  28.9 us
    broadcast_in_dim x2, other arithmetic, shards(): return (averaged[None], losses[None])  11 us
    all_to_all x2, starting transfers between devices, copy_for_each(): return lax.all_to_all(copies, axis, split_axis=0, concat_axis=0, tiled=True)  8.53 us
  transfers between devices with their start and end apart: 3, of which 3 were waited for; matrix products, arithmetic and copies ran while one was open for 0% of the time, Pallas kernels for 0%

commit v1 on v0

v1 whole, which is shorter than its diff:
```python
import functools

import jax
import jax.numpy as jnp
from jax import lax
from jax.experimental import pallas as pl
from jax.experimental.pallas import tpu as pltpu
from jax.sharding import PartitionSpec as P

beta_first = 0.9
beta_second = 0.95
learn_rate = 0.05
decay_rate = 0.1
adam_eps = 1e-05
norm_eps = 1e-06

F32 = jnp.float32
BF16 = jnp.bfloat16
MESH = pl.DeviceIdType.MESH
BLOCK = 256
LANES = 128
PARTS = 4


def kernel(
    exponent,
    width,
    order_ref,
    w_hbm,
    tok_hbm,
    cot_hbm,
    out_hbm,
    loss_ref,
    wv,
    tokv,
    cotv,
    hv,
    xt,
    w1,
    gb,
    dv,
    rcv,
    hop1,
    hop2,
    acc_s,
    acc_q,
    av,
    bv,
    stats,
    tok_sem,
    w_sem,
    c_sem,
    out_sem,
    st_send,
    st_recv,
    send_sem,
    recv_sem,
    hop_send,
    hop_recv,
):
    blocks = wv.shape[0]
    depth = wv.shape[1]
    tokens = hv.shape[1]
    quarter = depth // PARTS
    scale = depth ** (-0.5)
    eps = adam_eps / scale
    keep = 1.0 - learn_rate * decay_rate
    reps = lax.axis_size("rep")
    tps = lax.axis_size("tp")
    me = lax.axis_index("rep")
    mine = lax.axis_index("tp")
    dist = 2**exponent
    relayed = exponent in (1, 3)

    def ring(rep, by):
        place = lax.rem(lax.div(rep, dist), 4)
        return rep - dist * place + dist * lax.rem(place + by, 4)

    target = lax.rem(me + dist, reps)
    source = lax.rem(me + reps - dist, reps)
    partners = [{"rep": target}, {"rep": source}]
    if relayed:
        behind = ring(me, 3)
        entry = ring(target, 2)
        enters = lax.rem(ring(me, 2) + reps - dist, reps)
        partners += [{"rep": behind}, {"rep": ring(me, 1)}]
        partners += [{"rep": entry}, {"rep": enters}]
    partners += [{"tp": lax.rem(mine + k, tps)} for k in range(1, tps)]

    barrier = pltpu.get_barrier_semaphore()
    for partner in partners:
        pl.semaphore_signal(barrier, inc=1, device_id=partner, device_id_type=MESH)

    first, second = order_ref[0], order_ref[1]

    def columns(n):
        return pl.ds(pl.multiple_of(n * BLOCK, BLOCK), BLOCK)

    def w_copy(n):
        return pltpu.make_async_copy(w_hbm.at[:, columns(n)], wv.at[n], w_sem.at[n])

    def cotangent(n, chosen, half):
        at = pl.ds(pl.multiple_of(n * BLOCK + half * LANES, LANES), LANES)
        return cotv[chosen, :, at].astype(F32)

    tok_copy = pltpu.make_async_copy(tok_hbm, tokv, tok_sem)
    cot_copy = pltpu.make_async_copy(cot_hbm, cotv, c_sem)
    tok_copy.start()
    w_copy(0).start()
    cot_copy.start()
    w_copy(1).start()
    acc_s[...] = jnp.zeros_like(acc_s)
    acc_q[...] = jnp.zeros_like(acc_q)
    tok_copy.wait()

    def add_stats(n, chosen):
        for half in range(BLOCK // LANES):
            at = slice(half * LANES, (half + 1) * LANES)
            part = hv[n, :, at]
            acc_s[...] += part * part
            acc_q[...] += part * cotangent(n, chosen, half)

    def first_forward(n, carry):
        @pl.when(n + 2 < blocks)
        def _():
            w_copy(n + 2).start()

        w_copy(n).wait()
        hv[n] = jnp.dot(tokv[first], wv[n], preferred_element_type=F32)

        @pl.when(n == 0)
        def _():
            cot_copy.wait()

        add_stats(n, first)
        return carry

    lax.fori_loop(0, blocks, first_forward, 0)
    pl.semaphore_wait(barrier, len(partners))

    def exchange(step, chosen):
        stats[step, mine, 0:1, :] = jnp.sum(acc_s[...].T, axis=0, keepdims=True)
        stats[step, mine, 1:2, :] = jnp.sum(acc_q[...].T, axis=0, keepdims=True)
        copies = []
        for k in range(1, tps):
            copy = pltpu.make_async_remote_copy(
                src_ref=stats.at[step, mine],
                dst_ref=stats.at[step, mine],
                send_sem=st_send.at[step, k - 1],
                recv_sem=st_recv.at[step, k - 1],
                device_id={"tp": lax.rem(mine + k, tps)},
                device_id_type=MESH,
            )
            copy.start()
            copies.append(copy)
        acc_s[...] = jnp.zeros_like(acc_s)
        acc_q[...] = jnp.zeros_like(acc_q)
        for at in range(0, depth, BLOCK):
            xt[at : at + BLOCK, :] = tokv[chosen, :, at : at + BLOCK].T
        for copy in copies:
            copy.wait()
        total = stats[step, 0]
        for k in range(1, tps):
            total = total + stats[step, k]
        squares = total[0:1] * (scale * scale)
        inner = total[1:2] * scale
        radius = jnp.sqrt(squares / width + norm_eps)
        inverse = 1.0 / radius
        loss = jnp.sum(inner * inverse, axis=1, keepdims=True) / tokens
        loss_ref[step : step + 1, :] = jnp.broadcast_to(loss, (1, LANES))
        near = inverse * (1.0 / tokens)
        far = inner * inverse * inverse * inverse * (scale / (width * tokens))
        av[...] = jnp.broadcast_to(near, (LANES, tokens)).T
        bv[...] = jnp.broadcast_to(far, (LANES, tokens)).T

    def make_grad_rows(n, chosen):
        for half in range(BLOCK // LANES):
            at = slice(half * LANES, (half + 1) * LANES)
            rows = cotangent(n, chosen, half) * av[...] - hv[n, :, at] * bv[...]
            gb[:, at] = rows.astype(BF16)

    def first_update(grad):
        return grad / (jnp.abs(grad) + eps)

    exchange(0, first)

    def second_forward(n, carry):
        make_grad_rows(n, first)
        for r in range(depth // BLOCK):
            at = slice(r * BLOCK, (r + 1) * BLOCK)
            inside = slice((r * BLOCK) % quarter, (r * BLOCK) % quarter + BLOCK)
            grad = jnp.dot(xt[at, :], gb[...], preferred_element_type=F32)
            master = keep * wv[n, at, :].astype(F32) - learn_rate * first_update(grad)
            w1[at, :] = master.astype(BF16)
            dv[n, r * BLOCK // quarter, inside, :] = grad.astype(BF16)
        hv[n] = jnp.dot(tokv[second], w1[...], preferred_element_type=F32)
        add_stats(n, second)
        return carry

    lax.fori_loop(0, blocks, second_forward, 0)
    exchange(1, second)

    moment_old = beta_first * (1.0 - beta_first) / (1.0 - beta_first**2)
    moment_new = (1.0 - beta_first) / (1.0 - beta_first**2)
    second_old = beta_second * (1.0 - beta_second) / (1.0 - beta_second**2)
    second_new = (1.0 - beta_second) / (1.0 - beta_second**2)

    def direct(n, q):
        return pltpu.make_async_remote_copy(
            src_ref=dv.at[n, q],
            dst_ref=rcv.at[n, q],
            send_sem=send_sem.at[n, q],
            recv_sem=recv_sem.at[n, q],
            device_id={"rep": target},
            device_id_type=MESH,
        )

    def relay(stage, n):
        src = (dv.at[n, 0], hop1.at[n], hop2.at[n])[stage]
        dst = (hop1.at[n], hop2.at[n], rcv.at[n, 0])[stage]
        return pltpu.make_async_remote_copy(
            src_ref=src,
            dst_ref=dst,
            send_sem=hop_send.at[stage, n],
            recv_sem=recv_sem.at[n, 0] if stage == 2 else hop_recv.at[stage, n],
            device_id={"rep": entry if stage == 0 else behind},
            device_id_type=MESH,
        )

    def final_block(n, carry):
        make_grad_rows(n, second)
        for q in range(PARTS):

            def rows(r, inner_carry):
                inside = pl.ds(pl.multiple_of(r * BLOCK, BLOCK), BLOCK)
                at = pl.ds(pl.multiple_of(q * quarter + r * BLOCK, BLOCK), BLOCK)
                new = jnp.dot(xt[at, :], gb[...], preferred_element_type=F32)
                old = dv[n, q, inside, :].astype(F32)
                master = keep * wv[n, at, :].astype(F32) - learn_rate * first_update(old)
                top = moment_old * old + moment_new * new
                bottom = jnp.sqrt(second_old * old * old + second_new * new * new) + eps
                master = keep * master - learn_rate * (top / bottom)
                dv[n, q, inside, :] = master.astype(BF16)
                return inner_carry

            lax.fori_loop(0, quarter // BLOCK, rows, 0)
            if relayed and q == 0:
                relay(0, n).start()
            else:
                direct(n, q).start()
        return carry

    lax.fori_loop(0, blocks, final_block, 0)

    def out_copy(n, q):
        return pltpu.make_async_copy(
            rcv.at[n, q],
            out_hbm.at[q * quarter : (q + 1) * quarter, columns(n)],
            out_sem.at[n, q],
        )

    def average(n, q):
        for r in range(quarter // BLOCK):
            at = slice(r * BLOCK, (r + 1) * BLOCK)
            both = dv[n, q, at, :].astype(F32) + rcv[n, q, at, :].astype(F32)
            rcv[n, q, at, :] = (both * 0.5).astype(BF16)
        out_copy(n, q).start()

    def receive(k, carry):
        for t in range(PARTS - 1):
            if relayed:
                item = k * (PARTS - 1) + t

                @pl.when(item < blocks)
                def _():
                    relay(0, item).wait_recv()
                    relay(1, item).start()

                @pl.when((item >= blocks) & (item < 2 * blocks))
                def _():
                    relay(1, item - blocks).wait_recv()
                    relay(2, item - blocks).start()

                @pl.when(item >= 2 * blocks)
                def _():
                    relay(2, item - 2 * blocks).wait_recv()
                    average(item - 2 * blocks, 0)

            direct(k, t + 1).wait_recv()
            average(k, t + 1)
        if not relayed:
            direct(k, 0).wait_recv()
            average(k, 0)
        return carry

    lax.fori_loop(0, blocks, receive, 0)

    def finish(n, carry):
        for q in range(PARTS):
            if relayed and q == 0:
                for stage in range(3):
                    relay(stage, n).wait_send()
            else:
                direct(n, q).wait_send()
            out_copy(n, q).wait()
        return carry

    lax.fori_loop(0, blocks, finish, 0)


def run(exponent, weight, tokens, cotangent, order):
    depth, width = weight.shape
    steps, count, _ = tokens.shape
    blocks = width // BLOCK
    tps = lax.axis_size("tp")
    quarter = depth // PARTS
    relayed = exponent in (1, 3)
    hop = (blocks, quarter, BLOCK) if relayed else (1, 16, LANES)
    anywhere = pl.BlockSpec(memory_space=pl.ANY)
    dma = pltpu.SemaphoreType.DMA
    flops = 8 * count * depth * width
    return pl.pallas_call(
        functools.partial(kernel, exponent, width * tps),
        out_shape=(
            jax.ShapeDtypeStruct((depth, width), BF16),
            jax.ShapeDtypeStruct((8, LANES), F32),
        ),
        in_specs=[pl.BlockSpec(memory_space=pltpu.SMEM), anywhere, anywhere, anywhere],
        out_specs=(anywhere, pl.BlockSpec(memory_space=pltpu.VMEM)),
        scratch_shapes=[
            pltpu.VMEM((blocks, depth, BLOCK), BF16),
            pltpu.VMEM((steps, count, depth), BF16),
            pltpu.VMEM((steps, count, width), BF16),
            pltpu.VMEM((blocks, count, BLOCK), F32),
            pltpu.VMEM((depth, count), BF16),
            pltpu.VMEM((depth, BLOCK), BF16),
            pltpu.VMEM((count, BLOCK), BF16),
            pltpu.VMEM((blocks, PARTS, quarter, BLOCK), BF16),
            pltpu.VMEM((blocks, PARTS, quarter, BLOCK), BF16),
            pltpu.VMEM(hop, BF16),
            pltpu.VMEM(hop, BF16),
            pltpu.VMEM((count, LANES), F32),
            pltpu.VMEM((count, LANES), F32),
            pltpu.VMEM((count, LANES), F32),
            pltpu.VMEM((count, LANES), F32),
            pltpu.VMEM((steps, tps, 8, count), F32),
            dma,
            dma((blocks,)),
            dma,
            dma((blocks, PARTS)),
            dma((steps, tps - 1)),
            dma((steps, tps - 1)),
            dma((blocks, PARTS)),
            dma((blocks, PARTS)),
            dma((3, blocks)),
            dma((2, blocks)),
        ],
        compiler_params=pltpu.CompilerParams(
            collective_id=exponent + 1,
            has_side_effects=True,
            vmem_limit_bytes=60 * 1024 * 1024,
        ),
        cost_estimate=pl.CostEstimate(
            flops=flops, bytes_accessed=4 * depth * width, transcendentals=0
        ),
        name=f"local_steps_{exponent}",
    )(order, weight, tokens, cotangent)


def shards(weight, tokens, cotangent, batch_order, step_index):
    levels = lax.axis_size("rep").bit_length() - 1
    level = step_index[0] % levels

    def branch(exponent):
        return lambda: run(exponent, weight[0], tokens[0], cotangent[0], batch_order[0])

    averaged, losses = lax.switch(level, [branch(exponent) for exponent in range(levels)])
    return (averaged[None], losses[: tokens.shape[1], 0][None])


def solution(mesh):
    placed = (
        P("rep", None, "tp"),
        P("rep", None, None, None),
        P("rep", None, None, "tp"),
        P("rep", None),
        P(),
    )
    return jax.shard_map(
        shards,
        mesh=mesh,
        in_specs=placed,
        out_specs=(P("rep", None, "tp"), P("rep", None)),
        check_vma=False,
    )
```

time: 275 us -> 204 us (0.74)
  Pallas kernels: 0 us -> 193 us
  waiting for transfers between devices: 165 us -> 0 us
  matrix products: 73.4 us -> 0 us
  other arithmetic: 12.4 us -> 0 us
  starting transfers between devices: 9.84 us -> 0 us
  between operations: 6.49 us -> 1.3 us
    pallas_call x0 -> x1, Pallas kernels: none -> 193 us  [run(): pl.pallas_call(functools.partial(kernel, exponent, width * tps), out_shap...]
    ppermute x1 -> x0, waiting for transfers between devices: 162 us -> none  [shifted_2(): lax.ppermute(array, axis, [(i, (i + by) % devices) for i in range(devices)])]
    dot_general x4 -> x0, matrix products: 73.4 us -> none  [the longest x2 44.4 us: run_chain(): lax.dot_general(inputs, grad_rows, (((0,), (0,)), ((), ())), preferred_el...]
    broadcast_in_dim x2 -> x0, other arithmetic: 11 us -> none  [shards(): return (averaged[None], losses[None])]
    all_to_all x2 -> x0, starting transfers between devices: 8.53 us -> none  [copy_for_each(): return lax.all_to_all(copies, axis, split_axis=0, concat_axis=0, tiled=True)]
    unnamed x10 -> x1, local copies, waits for them, and re-layouts: 3.06 us -> 6.6 us
    all_to_all x2 -> x0, waiting for transfers between devices: 3.03 us -> none  [copy_for_each(): return lax.all_to_all(copies, axis, split_axis=0, concat_axis=0, tiled=True)]
  transfers between devices with their start and end apart: 3 -> 0, of which waited for: 3 -> 0; matrix products, arithmetic and copies ran while one was open for 0% -> 0% of each run, Pallas kernels for 0% -> 0%
where the time goes in v1:
time: 204 us; the launch traced here: 203 us
  Pallas kernels  193 us (95%)
  local copies, waits for them, and re-layouts  7.23 us (4%)
    pallas_call x1, Pallas kernels, run(): pl.pallas_call(functools.partial(kernel, exponent, width * tps), out_shap...  193 us
    unnamed x1, local copies, waits for them, and re-layouts  6.6 us

profile of v1, /device:TPU:1, one launch (start us, length us, event | category | flops | bytes accessed | tf_op | source)
XLA Modules:
  0.0 202.5 jit_solution(9052423604555237951)
XLA Ops:
  1.3 194.0 %conditional.1 = ((bf16[2048,1792]{1,0:T(8,128)(2,1)}, f32[8,128]{1,0:T(8,128)S(1)})) conditional(s32[]{:T(128)} %clamp.3, (s32[1,2]{1,0:T(1,128)}, bf16[1,2048,1792]{2,1,0:T(8,128)(2,1)}, bf16[1,2,512,2048]{3,2,1,0:T(8,128)(2,1)}, bf16[1,2,512,1792]{3,2,1,0:T(8,128)(2,1)}) %tuple.37, (s32[1,2]{1,0:T(1,128)}, ...), branch_computations={%region_0.1_spmd, %region_1.2_spmd, %region_2.3_spmd, %region_3.4_... | conditional | flops 15032385536 | bytes 14680072 | solution.py:377
  2.1 192.8 %local_steps_4.1 = (bf16[2048,1792]{1,0:T(8,128)(2,1)}, f32[8,128]{1,0:T(8,128)S(1)}) custom-call(s32[2]{0:T(128)} %bitcast.43, bf16[2048,1792]{1,0:T(8,128)(2,1)} %bitcast.28, bf16[2,512,2048]{2,1,0:T(8,128)(2,1)} %bitcast.33, bf16[2,512,1792]{2,1,0:T(8,128)(2,1)} %bitcast.38), custom_call_target="tpu_custom_call" | custom-call | flops 15032385536 | bytes 14680064 | tf_op jit(solution)/shard_map/cond/branch_4_fun/local_steps_4/pallas_call | solution.py:322
  195.3 0.6 slice_reduce_fusion
  195.9 6.6 %copy.19 = bf16[1,2048,1792]{2,1,0:T(8,128)(2,1)} copy(bf16[1,2048,1792]{2,1,0:T(8,128)(2,1)} %bitcast.23) | data formatting | bytes 14680064

commit v2 on v1

--- a/solution.py
+++ b/solution.py
@@ -25,11 +25,11 @@
 def kernel(
     exponent,
     width,
-    order_ref,
+    order_hbm,
     w_hbm,
     tok_hbm,
     cot_hbm,
-    out_hbm,
+    out_ref,
     loss_ref,
     wv,
     tokv,
@@ -47,10 +47,11 @@
     av,
     bv,
     stats,
+    order_ref,
+    order_sem,
     tok_sem,
     w_sem,
     c_sem,
-    out_sem,
     st_send,
     st_recv,
     send_sem,
@@ -91,7 +92,8 @@
     for partner in partners:
         pl.semaphore_signal(barrier, inc=1, device_id=partner, device_id_type=MESH)
 
-    first, second = order_ref[0], order_ref[1]
+    order_copy = pltpu.make_async_copy(order_hbm, order_ref, order_sem)
+    order_copy.start()
 
     def columns(n):
         return pl.ds(pl.multiple_of(n * BLOCK, BLOCK), BLOCK)
@@ -107,16 +109,19 @@
     cot_copy = pltpu.make_async_copy(cot_hbm, cotv, c_sem)
     tok_copy.start()
     w_copy(0).start()
-    cot_copy.start()
     w_copy(1).start()
     acc_s[...] = jnp.zeros_like(acc_s)
     acc_q[...] = jnp.zeros_like(acc_q)
+    order_copy.wait()
+    first, second = order_ref[0], order_ref[1]
     tok_copy.wait()
-
-    def add_stats(n, chosen):
+    cot_copy.start()
+
+    def add_stats(hidden, n, chosen):
+        hv[n] = hidden
         for half in range(BLOCK // LANES):
             at = slice(half * LANES, (half + 1) * LANES)
-            part = hv[n, :, at]
+            part = hidden[:, at]
             acc_s[...] += part * part
             acc_q[...] += part * cotangent(n, chosen, half)
 
@@ -126,16 +131,15 @@
             w_copy(n + 2).start()
 
         w_copy(n).wait()
-        hv[n] = jnp.dot(tokv[first], wv[n], preferred_element_type=F32)
-
-        @pl.when(n == 0)
-        def _():
-            cot_copy.wait()
-
-        add_stats(n, first)
+        add_stats(jnp.dot(tokv[first], wv[n], preferred_element_type=F32), n, first)
         return carry
 
-    lax.fori_loop(0, blocks, first_forward, 0)
+    w_copy(2).start()
+    w_copy(0).wait()
+    hv[0] = jnp.dot(tokv[first], wv[0], preferred_element_type=F32)
+    cot_copy.wait()
+    add_stats(hv[0], 0, first)
+    lax.fori_loop(1, blocks, first_forward, 0)
     pl.semaphore_wait(barrier, len(partners))
 
     def exchange(step, chosen):
@@ -183,9 +187,9 @@
         return grad / (jnp.abs(grad) + eps)
 
     exchange(0, first)
+    make_grad_rows(0, first)
 
     def second_forward(n, carry):
-        make_grad_rows(n, first)
         for r in range(depth // BLOCK):
             at = slice(r * BLOCK, (r + 1) * BLOCK)
             inside = slice((r * BLOCK) % quarter, (r * BLOCK) % quarter + BLOCK)
@@ -193,8 +197,8 @@
             master = keep * wv[n, at, :].astype(F32) - learn_rate * first_update(grad)
             w1[at, :] = master.astype(BF16)
             dv[n, r * BLOCK // quarter, inside, :] = grad.astype(BF16)
-        hv[n] = jnp.dot(tokv[second], w1[...], preferred_element_type=F32)
-        add_stats(n, second)
+        make_grad_rows(jnp.minimum(n + 1, blocks - 1), first)
+        add_stats(jnp.dot(tokv[second], w1[...], preferred_element_type=F32), n, second)
         return carry
 
     lax.fori_loop(0, blocks, second_forward, 0)
@@ -229,8 +233,8 @@
 
     def final_block(n, carry):
         make_grad_rows(n, second)
-        for q in range(PARTS):
-
+
+        def part(q, part_carry):
             def rows(r, inner_carry):
                 inside = pl.ds(pl.multiple_of(r * BLOCK, BLOCK), BLOCK)
                 at = pl.ds(pl.multiple_of(q * quarter + r * BLOCK, BLOCK), BLOCK)
@@ -244,27 +248,32 @@
                 return inner_carry
 
             lax.fori_loop(0, quarter // BLOCK, rows, 0)
-            if relayed and q == 0:
-                relay(0, n).start()
+            if relayed:
+
+                @pl.when(q == 0)
+                def _():
+                    relay(0, n).start()
+
+                @pl.when(q > 0)
+                def _():
+                    direct(n, q).start()
+
             else:
                 direct(n, q).start()
+            return part_carry
+
+        lax.fori_loop(0, PARTS, part, 0)
         return carry
 
     lax.fori_loop(0, blocks, final_block, 0)
-
-    def out_copy(n, q):
-        return pltpu.make_async_copy(
-            rcv.at[n, q],
-            out_hbm.at[q * quarter : (q + 1) * quarter, columns(n)],
-            out_sem.at[n, q],
-        )
 
     def average(n, q):
         for r in range(quarter // BLOCK):
             at = slice(r * BLOCK, (r + 1) * BLOCK)
             both = dv[n, q, at, :].astype(F32) + rcv[n, q, at, :].astype(F32)
-            rcv[n, q, at, :] = (both * 0.5).astype(BF16)
-        out_copy(n, q).start()
+            out_ref[q * quarter + r * BLOCK : q * quarter + (r + 1) * BLOCK, columns(n)] = (
+                both * 0.5
+            ).astype(BF16)
 
     def receive(k, carry):
         for t in range(PARTS - 1):
@@ -302,7 +311,6 @@
                     relay(stage, n).wait_send()
             else:
                 direct(n, q).wait_send()
-            out_copy(n, q).wait()
         return carry
 
     lax.fori_loop(0, blocks, finish, 0)
@@ -322,11 +330,11 @@
     return pl.pallas_call(
         functools.partial(kernel, exponent, width * tps),
         out_shape=(
-            jax.ShapeDtypeStruct((depth, width), BF16),
+            pltpu.VMEM((depth, width), BF16),
             jax.ShapeDtypeStruct((8, LANES), F32),
         ),
-        in_specs=[pl.BlockSpec(memory_space=pltpu.SMEM), anywhere, anywhere, anywhere],
-        out_specs=(anywhere, pl.BlockSpec(memory_space=pltpu.VMEM)),
+        in_specs=[anywhere] * 4,
+        out_specs=(pl.BlockSpec(memory_space=pltpu.VMEM),) * 2,
         scratch_shapes=[
             pltpu.VMEM((blocks, depth, BLOCK), BF16),
             pltpu.VMEM((steps, count, depth), BF16),
@@ -344,10 +352,11 @@
             pltpu.VMEM((count, LANES), F32),
             pltpu.VMEM((count, LANES), F32),
             pltpu.VMEM((steps, tps, 8, count), F32),
+            pltpu.SMEM((steps,), jnp.int32),
+            dma,
             dma,
             dma((blocks,)),
             dma,
-            dma((blocks, PARTS)),
             dma((steps, tps - 1)),
             dma((steps, tps - 1)),
             dma((blocks, PARTS)),
@@ -358,7 +367,7 @@
         compiler_params=pltpu.CompilerParams(
             collective_id=exponent + 1,
             has_side_effects=True,
-            vmem_limit_bytes=60 * 1024 * 1024,
+            vmem_limit_bytes=48 * 1024 * 1024,
         ),
         cost_estimate=pl.CostEstimate(
             flops=flops, bytes_accessed=4 * depth * width, transcendentals=0

time: 204 us -> 160 us (0.78)
  Pallas kernels: 193 us -> 154 us
  local copies, waits for them, and re-layouts: 7.23 us -> 3.67 us
    pallas_call x1, Pallas kernels: 193 us -> 154 us  [run(): pl.pallas_call(functools.partial(kernel, exponent, width * tps), out_shap...]
    unnamed x1, local copies, waits for them, and re-layouts: 6.6 us -> 3.05 us
where the time goes in v2:
time: 160 us; the launch traced here: 159 us
  Pallas kernels  154 us (96%)
  local copies, waits for them, and re-layouts  3.67 us (2%)
    pallas_call x1, Pallas kernels, run(): pl.pallas_call(functools.partial(kernel, exponent, width * tps), out_shap...  154 us

profile of v2, /device:TPU:1, one launch (start us, length us, event | category | flops | bytes accessed | tf_op | source)
XLA Modules:
  0.0 159.0 jit_solution(10723256684063758714)
XLA Ops:
  1.3 154.0 %conditional.1 = ((bf16[2048,1792]{1,0:T(8,128)(2,1)S(1)}, f32[8,128]{1,0:T(8,128)S(1)})) conditional(s32[]{:T(128)} %clamp.3, (s32[1,2]{1,0:T(1,128)}, bf16[1,2048,1792]{2,1,0:T(8,128)(2,1)}, bf16[1,2,512,2048]{3,2,1,0:T(8,128)(2,1)}, bf16[1,2,512,1792]{3,2,1,0:T(8,128)(2,1)}) %tuple.37, (s32[1,2]{1,0:T(1,128)}, ...), branch_computations={%region_0.1_spmd, %region_1.2_spmd, %region_2.3_spmd, %region_3.4_... | conditional | flops 15032385536 | bytes 14680072 | solution.py:386
  1.5 153.6 %local_steps_3.1 = (bf16[2048,1792]{1,0:T(8,128)(2,1)S(1)}, f32[8,128]{1,0:T(8,128)S(1)}) custom-call(s32[2]{0:T(128)} %bitcast.42, bf16[2048,1792]{1,0:T(8,128)(2,1)} %bitcast.27, bf16[2,512,2048]{2,1,0:T(8,128)(2,1)} %bitcast.32, bf16[2,512,1792]{2,1,0:T(8,128)(2,1)} %bitcast.37), custom_call_target="tpu_custom_call" | custom-call | flops 15032385536 | bytes 14680064 | tf_op jit(solution)/shard_map/cond/branch_3_fun/local_steps_3/pallas_call | solution.py:330
  155.3 0.6 slice_reduce_fusion
  156.0 3.0 %copy.18 = bf16[1,2048,1792]{2,1,0:T(8,128)(2,1)} copy(bf16[1,2048,1792]{2,1,0:T(8,128)(2,1)S(1)} %bitcast.23) | data formatting | bytes 14680064
